TPU v7x, 256 devices: a whole 4x4x8 slice. The times are simulated.
256 devices in a mesh: seq: 128 (over z, y_hi, x, core), exp: 2 (over y_lo).
Axes of the slice: x: 4, y: 4 (y_hi: 2, y_lo: 2; y = y_hi * 2 + y_lo), z: 8, core: 2. Of those that a mesh axis runs over, the one named last changes fastest.
Arguments:
- queries: bfloat16 [49152, 1536], P('seq', 'exp'), may hold values from -120 to 120
- key_heads: bfloat16 [49152, 1536], P('seq', 'exp'), may hold values from -6 to 6
- value_heads: bfloat16 [49152, 1024], P('seq', 'exp'), may hold values from -6 to 6
- block_layout: int32 [384, 16], P('seq'), may hold values from 0 to 21, as said below
- out_weight: bfloat16 [1024, 2048], P('exp'), may hold values from -0.1875 to 0.1875
- norm_gain: float32 [2048], replicated, may hold values from 0.5 to 1.5
- expert_ids: int32 [49152, 1], P(('seq', 'exp')), may hold values from 0 to 1; in each aligned block of 192 rows (0 to 191, 192 to 383, ...) at most 144 rows name the same one
- route_weight: float32 [49152, 1], P(('seq', 'exp')), may hold values from 0.1 to 1
- gate_weight: bfloat16 [2, 2048, 704], P('exp'), may hold values from -0.125 to 0.125
- up_weight: bfloat16 [2, 2048, 704], P('exp'), may hold values from -0.125 to 0.125
- down_weight: bfloat16 [2, 704, 2048], P('exp'), may hold values from -0.21875 to 0.21875
Outputs:
- layer_out: bfloat16 [49152, 2048], P(('seq', 'exp'))
Inputs may be any that keep to these rules, and one draw needn't show every extreme that they name: `block_layout`: each row holds the offset 0 and 15 other distinct offsets. `expert_ids`: among the 192 tokens of one device in the expert layer (aligned blocks of rows) at most 144 name the same expert.
All inputs are finite; a program needn't handle non-finite values.
Results may differ from a plain program's by a relative error of at most 0.02.
Values may be sent and summed in bfloat16 or wider, within the bound.
A program may use at most 128 MiB of HBM per device.

v0:
```python
import jax
import jax.numpy as jnp
from jax import lax
from jax.sharding import PartitionSpec as P

QK = 192
VD = 128
BLK = 128
REACH = 8


def shifted(array, axis, by):
    peers = lax.axis_size(axis)
    pairs = [(i, i + by) for i in range(peers) if 0 <= i + by < peers]
    return lax.ppermute(array, axis, pairs)


def cut_along(array, dim, peers):
    dims = array.shape
    pieces = array.reshape(*dims[:dim], peers, dims[dim] // peers, *dims[dim + 1 :])
    return jnp.moveaxis(pieces, dim, 0)


def sum_at_owner(array, axis, dim):
    pieces = cut_along(array, dim, lax.axis_size(axis))
    arrived = lax.all_to_all(pieces, axis, split_axis=0, concat_axis=0, tiled=True)
    return arrived.astype(jnp.float32).sum(axis=0)


def expert_apply(arrivals, gate_matrix, up_matrix, down_matrix):
    gate_part = jnp.dot(arrivals, gate_matrix, preferred_element_type=jnp.float32)
    up_part = jnp.dot(arrivals, up_matrix, preferred_element_type=jnp.float32)
    hidden = (jax.nn.silu(gate_part) * up_part).astype(jnp.bfloat16)
    return jnp.dot(hidden, down_matrix, preferred_element_type=jnp.float32).astype(jnp.bfloat16)


def shards(
    queries,
    key_heads,
    value_heads,
    block_layout,
    out_weight,
    norm_gain,
    expert_ids,
    route_weight,
    gate_weight,
    up_weight,
    down_weight,
):
    tok_seq = queries.shape[0]
    blocks_here = tok_seq // BLK
    heads_here = value_heads.shape[1] // VD
    key_width = key_heads.shape[1]
    chosen = block_layout.shape[1]
    seq_index = lax.axis_index("seq")
    packed = jnp.concatenate([key_heads, value_heads], axis=1)
    pieces = [packed]
    carried = packed
    for distance in range(REACH - 1):
        carried = shifted(carried, "seq", 1)
        pieces.append(carried)
    window = jnp.concatenate(pieces[::-1], axis=0).reshape(
        REACH * blocks_here, BLK, packed.shape[1]
    )
    local_block = jnp.arange(blocks_here, dtype=jnp.int32)[:, None]
    position = local_block + (REACH - 1) * blocks_here - block_layout
    anchor = seq_index * blocks_here + local_block - block_layout
    picked = jnp.take(window, position.reshape(-1), axis=0).reshape(
        blocks_here, chosen * BLK, packed.shape[1]
    )
    keys_sel = picked[:, :, :key_width].reshape(blocks_here, chosen * BLK, heads_here, QK)
    values_sel = picked[:, :, key_width:].reshape(blocks_here, chosen * BLK, heads_here, VD)
    query_grid = queries.reshape(blocks_here, BLK, heads_here, QK)
    scores = jnp.einsum(
        "bqhd,bkhd->bhqk", query_grid, keys_sel, preferred_element_type=jnp.float32
    ) * QK ** (-0.5)
    within = jnp.arange(BLK, dtype=jnp.int32)
    query_pos = (seq_index * blocks_here + local_block) * BLK + within[None, :]
    key_pos = (anchor[:, :, None] * BLK + within[None, None, :]).reshape(blocks_here, chosen * BLK)
    key_valid = jnp.repeat(anchor >= 0, BLK, axis=1)
    allowed = key_valid[:, None, :] & (key_pos[:, None, :] <= query_pos[:, :, None])
    scores = jnp.where(allowed[:, None], scores, jnp.float32(-1e30))
    row_peak = jnp.max(scores, axis=3, keepdims=True)
    weights = jnp.exp(scores - row_peak)
    attn_probs = (weights / jnp.sum(weights, axis=3, keepdims=True)).astype(jnp.bfloat16)
    context = jnp.einsum(
        "bhqk,bkhd->bqhd", attn_probs, values_sel, preferred_element_type=jnp.float32
    )
    context = context.astype(jnp.bfloat16).reshape(tok_seq, heads_here * VD)
    groups = lax.axis_size("exp")
    tok_dev = tok_seq // groups
    attended = sum_at_owner(
        jnp.dot(context, out_weight, preferred_element_type=jnp.float32).astype(jnp.bfloat16),
        "exp",
        0,
    )
    rescale = lax.rsqrt(jnp.mean(attended * attended, axis=1, keepdims=True) + 1e-06)
    normed = (attended * rescale * norm_gain).astype(jnp.bfloat16)
    capacity = 3 * tok_dev // (2 * groups)
    route_ids = expert_ids[:, 0]
    member = (route_ids[:, None] == jnp.arange(groups, dtype=jnp.int32)[None, :]).astype(jnp.int32)
    slot_rank = jnp.sum((jnp.cumsum(member, axis=0) - 1) * member, axis=1)
    target = route_ids * capacity + slot_rank
    placement = (jnp.arange(groups * capacity, dtype=jnp.int32)[:, None] == target[None, :]).astype(
        jnp.bfloat16
    )
    outgoing = jnp.dot(placement, normed, preferred_element_type=jnp.float32).astype(jnp.bfloat16)
    outgoing = outgoing.reshape(groups, capacity, normed.shape[1])
    arrived = lax.all_to_all(outgoing, "exp", split_axis=0, concat_axis=0, tiled=True)
    stacked = arrived.reshape(-1, arrived.shape[2])
    result = expert_apply(stacked, gate_weight[0], up_weight[0], down_weight[0]).reshape(
        arrived.shape
    )
    returned = lax.all_to_all(result, "exp", split_axis=0, concat_axis=0, tiled=True)
    gathered = lax.dot_general(
        placement,
        returned.reshape(groups * capacity, -1),
        (((0,), (0,)), ((), ())),
        preferred_element_type=jnp.float32,
    )
    return (attended + route_weight * gathered).astype(jnp.bfloat16)


def solution(mesh):
    in_specs = (
        P("seq", "exp"),
        P("seq", "exp"),
        P("seq", "exp"),
        P("seq", None),
        P("exp", None),
        P(),
        P(("seq", "exp"), None),
        P(("seq", "exp"), None),
        P("exp", None, None),
        P("exp", None, None),
        P("exp", None, None),
    )
    out_specs = P(("seq", "exp"), None)
    return jax.shard_map(shards, mesh=mesh, in_specs=in_specs, out_specs=out_specs, check_vma=False)
```

profile of v0, /device:TPU:128, one launch (start us, length us, event | category | flops | bytes accessed | tf_op | source)
XLA Modules:
  0.0 332.3 jit_solution(9788490452917607852)
XLA Ops:
  1.4 1.9 collective-permute-start
  3.3 19.2 %collective-permute-done = bf16[384,1280]{1,0:T(8,128)(2,1)S(1)} collective-permute-done((bf16[384,1280]{1,0:T(8,128)(2,1)S(1)}, bf16[384,1280]{1,0:T(8,128)(2,1)S(1)}, u32[]{:S(2)}, u32[]{:S(2)}) %collective-permute-start) | collective-permute-done | bytes 983072 | tf_op jit(solution)/shard_map/ppermute | solution.py:15
  25.5 19.2 %collective-permute-done.1 = bf16[384,1280]{1,0:T(8,128)(2,1)S(1)} collective-permute-done((bf16[384,1280]{1,0:T(8,128)(2,1)S(1)}, bf16[384,1280]{1,0:T(8,128)(2,1)S(1)}, u32[]{:S(2)}, u32[]{:S(2)}) %collective-permute-start.1) | collective-permute-done | bytes 983072 | tf_op jit(solution)/shard_map/ppermute | solution.py:15
  47.6 19.2 %collective-permute-done.2 = bf16[384,1280]{1,0:T(8,128)(2,1)S(1)} collective-permute-done((bf16[384,1280]{1,0:T(8,128)(2,1)S(1)}, bf16[384,1280]{1,0:T(8,128)(2,1)S(1)}, u32[]{:S(2)}, u32[]{:S(2)}) %collective-permute-start.2) | collective-permute-done | bytes 983072 | tf_op jit(solution)/shard_map/ppermute | solution.py:15
  69.7 19.3 %collective-permute-done.3 = bf16[384,1280]{1,0:T(8,128)(2,1)} collective-permute-done((bf16[384,1280]{1,0:T(8,128)(2,1)S(1)}, bf16[384,1280]{1,0:T(8,128)(2,1)}, u32[]{:S(2)}, u32[]{:S(2)}) %collective-permute-start.3) | collective-permute-done | bytes 983072 | tf_op jit(solution)/shard_map/ppermute | solution.py:15
  91.9 2.9 reshape.158
  94.9 15.5 %collective-permute-done.4 = bf16[384,1280]{1,0:T(8,128)(2,1)} collective-permute-done((bf16[384,1280]{1,0:T(8,128)(2,1)}, bf16[384,1280]{1,0:T(8,128)(2,1)}, u32[]{:S(2)}, u32[]{:S(2)}) %collective-permute-start.4) | collective-permute-done | bytes 983072 | tf_op jit(solution)/shard_map/ppermute | solution.py:15
  113.3 18.5 %collective-permute-done.5 = bf16[384,1280]{1,0:T(8,128)(2,1)S(1)} collective-permute-done((bf16[384,1280]{1,0:T(8,128)(2,1)}, bf16[384,1280]{1,0:T(8,128)(2,1)S(1)}, u32[]{:S(2)}, u32[]{:S(2)}) %collective-permute-start.5) | collective-permute-done | bytes 983072 | tf_op jit(solution)/shard_map/ppermute | solution.py:15
  131.8 2.1 collective-permute-start.6
  133.9 4.0 %compare_and_fusion = pred[3,128,2048]{1,2,0:T(8,128)(4,1)} fusion(s32[3,128]{1,0:T(4,128)S(1)} %iota_add_fusion, s32[3,2048]{1,0:T(4,128)S(1)} %bitcast_add_fusion, pred[3,2048]{1,0:T(4,128)(4,1)S(1)} %bitcast.92), kind=kLoop, calls=%fused_computation.12 | loop fusion | flops 1572864 | bytes 818688 | tf_op jit(solution)/shard_map/and | solution.py:81
  137.9 15.0 %collective-permute-done.6 = bf16[384,1280]{1,0:T(8,128)(2,1)S(1)} collective-permute-done((bf16[384,1280]{1,0:T(8,128)(2,1)S(1)}, bf16[384,1280]{1,0:T(8,128)(2,1)S(1)}, u32[]{:S(2)}, u32[]{:S(2)}) %collective-permute-start.6) | collective-permute-done | bytes 983072 | tf_op jit(solution)/shard_map/ppermute | solution.py:15
  155.0 2.2 constant_dynamic-update-slice_fusion.5
  157.2 2.2 constant_dynamic-update-slice_fusion.4
  164.2 10.7 %gather_fusion = bf16[48,128,1280]{2,1,0:T(8,128)(2,1)} fusion(bf16[24,128,1280]{2,1,0:T(8,128)(2,1)} %bitcast, s32[1024]{0:T(1024)S(1)} %pad_clamp_fusion), kind=kCustom, calls=%fused_computation | custom fusion | bytes 31457472 | tf_op jit(solution)/shard_map/jit(_take)/gather | solution.py:68
  174.9 8.2 %bitcast_select_fusion = bf16[3,2048,1280]{2,1,0:T(8,128)(2,1)S(1)} fusion(pred[3,2048]{1,0:T(4,128)(4,1)S(1)} %bitcast.91, bf16[3,2048,1280]{2,1,0:T(8,128)(2,1)} %bitcast.81), kind=kLoop, calls=%fused_computation.2 | loop fusion | flops 7864320 | bytes 31463424 | tf_op jit(solution)/shard_map/jit(_take)/select_n | solution.py:68
  183.2 5.6 %copy-done.1 = bf16[3,2048,1280]{2,1,0:T(8,128)(2,1)} copy-done((bf16[3,2048,1280]{2,1,0:T(8,128)(2,1)}, bf16[3,2048,1280]{2,1,0:T(8,128)(2,1)S(1)}, u32[]{:S(2)}) %copy-start.1) | copy-done | bytes 15728664
  188.7 3.2 slice.22
  191.9 7.9 %slice.23 = bf16[3,2048,768]{2,1,0:T(8,128)(2,1)} slice(bf16[3,2048,1280]{2,1,0:T(8,128)(2,1)} %copy-done.1), slice={[0:3], [0:2048], [0:768]} | slice | bytes 18874368 | tf_op jit(solution)/shard_map/slice | solution.py:71
  199.8 8.9 %copy.14 = bf16[3,2048,512]{1,2,0:T(8,128)(2,1)} copy(bf16[3,2048,512]{2,1,0:T(8,128)(2,1)} %slice.22) | data formatting | bytes 12582912 | tf_op jit(solution)/shard_map/slice | solution.py:72
  208.7 12.7 %copy.15 = bf16[3,2048,768]{1,2,0:T(8,128)(2,1)} copy(bf16[3,2048,768]{2,1,0:T(8,128)(2,1)} %slice.23) | data formatting | bytes 18874368 | tf_op jit(solution)/shard_map/slice | solution.py:71
  221.4 12.3 %fusion.25 = f32[3,4,2048,128]{3,2,1,0:T(8,128)} fusion(bf16[3,2048,4,192]{1,3,2,0:T(8,128)(2,1)} %bitcast.82, bf16[3,128,4,192]{3,2,1,0:T(4,128)(2,1)} %reshape.158), kind=kOutput, calls=%fused_computation.32 | convolution fusion | flops 1207959552 | bytes 22609920 | tf_op jit(solution)/shard_map/bqhd,bkhd->bhqk/dot_general | solution.py:74
  233.7 17.3 %fusion.41 = (f32[3,4,128]{2,1,0:T(4,128)S(1)}, f32[3,4,128,2048]{2,3,1,0:T(8,128)}) fusion(f32[3,4,2048,128]{3,2,1,0:T(8,128)} %fusion.25, pred[3,128,2048]{1,2,0:T(8,128)(4,1)} %compare_and_fusion), kind=kOutput, calls=%fused_computation.83 | output fusion | flops 18876416 | bytes 25958400 | tf_op jit(solution)/shard_map/sub | solution.py:84
  251.0 8.3 %fusion.24 = bf16[3,128,4,128]{1,3,2,0:T(8,128)(2,1)S(1)} fusion(bf16[3,2048,4,128]{1,3,2,0:T(8,128)(2,1)} %bitcast.83, f32[3,4,128,2048]{2,3,1,0:T(8,128)} %get-tuple-element.9, f32[3,4,128]{2,1,0:T(4,128)S(1)} %get-tuple-element.8), kind=kOutput, calls=%fused_computation.30 | convolution fusion | flops 811794432 | bytes 19273728 | tf_op jit(solution)/shard_map/bhqk,bkhd->bqhd/dot_general | solution.py:86
  260.3 3.9 %convolution_convert_fusion = bf16[384,2048]{1,0:T(8,128)(2,1)} fusion(bf16[512,2048]{1,0:T(8,128)(2,1)} %param.15, bf16[48,8,4,128]{3,2,1,0:T(4,128)(2,1)} %bitcast.90), kind=kOutput, calls=%fused_computation.19 | convolution fusion | flops 806092800 | bytes 4063232 | tf_op jit(solution)/shard_map/dot_general | solution.py:93
  264.2 4.6 %all-to-all-start = ((bf16[2,192,2048]{2,1,0:T(8,128)(2,1)}), bf16[2,192,2048]{2,1,0:T(8,128)(2,1)}, u32[]{:S(2)}, u32[]{:S(2)}) async-start(bf16[2,192,2048]{2,1,0:T(8,128)(2,1)} %bitcast.86), calls=%async_computation | async-start | bytes 3145728 | tf_op jit(solution)/shard_map/all_to_all | solution.py:26
  270.0 17.2 %all-to-all-done = bf16[2,192,2048]{2,1,0:T(8,128)(2,1)} async-done(((bf16[2,192,2048]{2,1,0:T(8,128)(2,1)}), bf16[2,192,2048]{2,1,0:T(8,128)(2,1)}, u32[]{:S(2)}, u32[]{:S(2)}) %all-to-all-start) | async-done | bytes 1572896 | tf_op jit(solution)/shard_map/all_to_all | solution.py:26
  287.2 2.1 convert_reduce_fusion
  291.0 15.8 %all_to_all.15 = bf16[2,144,2048]{2,1,0:T(8,128)(2,1)S(1)} all-to-all(bf16[2,144,2048]{2,1,0:T(8,128)(2,1)S(1)} %bitcast.85), channel_id=1, replica_groups=mesh['seq'=128,'exp'=2] {'exp'}, dimensions={0} | all-to-all | bytes 2359296 | tf_op jit(solution)/shard_map/all_to_all | solution.py:109
  307.9 2.1 fusion.10
  309.9 5.8 %fusion.12 = bf16[288,2048]{1,0:T(8,128)(2,1)} fusion(bf16[1,704,2048]{2,1,0:T(8,128)(2,1)S(1)} %copy-done, bf16[288,2048]{1,0:T(8,128)(2,1)} %bitcast.88, bf16[1,2048,704]{1,2,0:T(8,128)(2,1)} %param.20, f32[288,704]{1,0:T(8,128)} %fusion.10), kind=kOutput, calls=%fused_computation.21 | convolution fusion | flops 1662750720 | bytes 8937472 | tf_op jit(solution)/shard_map/dot_general | solution.py:34
  315.7 13.7 %all_to_all.16 = bf16[2,144,2048]{2,1,0:T(8,128)(2,1)S(1)} all-to-all(bf16[2,144,2048]{2,1,0:T(8,128)(2,1)} %bitcast.89), channel_id=1, replica_groups=mesh['seq'=128,'exp'=2] {'exp'}, dimensions={0} | all-to-all | bytes 2359296 | tf_op jit(solution)/shard_map/all_to_all | solution.py:114
  329.4 2.9 fusion.16
  (73 shorter events, 27.6 us)
Async XLA Ops:
  0.0 309.9 %copy-start = (bf16[1,704,2048]{2,1,0:T(8,128)(2,1)S(1)}, bf16[1,704,2048]{2,1,0:T(8,128)(2,1)}, u32[]{:S(2)}) copy-start(bf16[1,704,2048]{2,1,0:T(8,128)(2,1)} %param.21) | copy-start | bytes 8650756
  1.4 21.1 %collective-permute-start = (bf16[384,1280]{1,0:T(8,128)(2,1)S(1)}, bf16[384,1280]{1,0:T(8,128)(2,1)S(1)}, u32[]{:S(2)}, u32[]{:S(2)}) collective-permute-start(bf16[384,1280]{1,0:T(8,128)(2,1)S(1)} %pad_maximum_fusion), channel_id=1, source_target_pairs={{0,2},{2,4},{4,6},{6,8},{8,10},{10,12},{12,14},{14,16},{16,18},{18... | collective-permute-start | bytes 2949128 | tf_op jit(solution)/shard_map/ppermute | solution.py:15
  22.5 1.0 copy-start.6
  23.6 21.1 %collective-permute-start.1 = (bf16[384,1280]{1,0:T(8,128)(2,1)S(1)}, bf16[384,1280]{1,0:T(8,128)(2,1)S(1)}, u32[]{:S(2)}, u32[]{:S(2)}) collective-permute-start(bf16[384,1280]{1,0:T(8,128)(2,1)S(1)} %collective-permute-done), channel_id=1, source_target_pairs={{0,2},{2,4},{4,6},{6,8},{8,10},{10,12},{12,14},{14,16},{16,18},{18... | collective-permute-start | bytes 2949128 | tf_op jit(solution)/shard_map/ppermute | solution.py:15
  44.7 0.9 copy-start.8
  45.7 21.1 %collective-permute-start.2 = (bf16[384,1280]{1,0:T(8,128)(2,1)S(1)}, bf16[384,1280]{1,0:T(8,128)(2,1)S(1)}, u32[]{:S(2)}, u32[]{:S(2)}) collective-permute-start(bf16[384,1280]{1,0:T(8,128)(2,1)S(1)} %collective-permute-done.1), channel_id=1, source_target_pairs={{0,2},{2,4},{4,6},{6,8},{8,10},{10,12},{12,14},{14,16},{16,18},{18... | collective-permute-start | bytes 2949128 | tf_op jit(solution)/shard_map/ppermute | solution.py:15
  66.8 1.0 copy-start.10
  67.7 21.2 %collective-permute-start.3 = (bf16[384,1280]{1,0:T(8,128)(2,1)S(1)}, bf16[384,1280]{1,0:T(8,128)(2,1)}, u32[]{:S(2)}, u32[]{:S(2)}) collective-permute-start(bf16[384,1280]{1,0:T(8,128)(2,1)S(1)} %collective-permute-done.2), channel_id=1, source_target_pairs={{0,2},{2,4},{4,6},{6,8},{8,10},{10,12},{12,14},{14,16},{16,18},{18... | collective-permute-start | bytes 2949128 | tf_op jit(solution)/shard_map/ppermute | solution.py:15
  89.0 21.4 %collective-permute-start.4 = (bf16[384,1280]{1,0:T(8,128)(2,1)}, bf16[384,1280]{1,0:T(8,128)(2,1)}, u32[]{:S(2)}, u32[]{:S(2)}) collective-permute-start(bf16[384,1280]{1,0:T(8,128)(2,1)} %collective-permute-done.3), channel_id=1, source_target_pairs={{0,2},{2,4},{4,6},{6,8},{8,10},{10,12},{12,14},{14,16},{16,18},{18... | collective-permute-start | bytes 2949128 | tf_op jit(solution)/shard_map/ppermute | solution.py:15
  94.8 64.6 %copy-start.11 = (bf16[384,1280]{1,0:T(8,128)(2,1)S(1)}, bf16[384,1280]{1,0:T(8,128)(2,1)}, u32[]{:S(2)}) copy-start(bf16[384,1280]{1,0:T(8,128)(2,1)} %copy-done.10) | copy-start | bytes 2949124
  94.8 65.7 %copy-start.9 = (bf16[384,1280]{1,0:T(8,128)(2,1)S(1)}, bf16[384,1280]{1,0:T(8,128)(2,1)}, u32[]{:S(2)}) copy-start(bf16[384,1280]{1,0:T(8,128)(2,1)} %copy-done.8) | copy-start | bytes 2949124
  110.4 21.3 %collective-permute-start.5 = (bf16[384,1280]{1,0:T(8,128)(2,1)}, bf16[384,1280]{1,0:T(8,128)(2,1)S(1)}, u32[]{:S(2)}, u32[]{:S(2)}) collective-permute-start(bf16[384,1280]{1,0:T(8,128)(2,1)} %collective-permute-done.4), channel_id=1, source_target_pairs={{0,2},{2,4},{4,6},{6,8},{8,10},{10,12},{12,14},{14,16},{16,18},{18... | collective-permute-start | bytes 2949128 | tf_op jit(solution)/shard_map/ppermute | solution.py:15
  131.8 21.1 %collective-permute-start.6 = (bf16[384,1280]{1,0:T(8,128)(2,1)S(1)}, bf16[384,1280]{1,0:T(8,128)(2,1)S(1)}, u32[]{:S(2)}, u32[]{:S(2)}) collective-permute-start(bf16[384,1280]{1,0:T(8,128)(2,1)S(1)} %collective-permute-done.5), channel_id=1, source_target_pairs={{0,2},{2,4},{4,6},{6,8},{8,10},{10,12},{12,14},{14,16},{16,18},{18... | collective-permute-start | bytes 2949128 | tf_op jit(solution)/shard_map/ppermute | solution.py:15
  133.9 27.6 %copy-start.7 = (bf16[384,1280]{1,0:T(8,128)(2,1)S(1)}, bf16[384,1280]{1,0:T(8,128)(2,1)}, u32[]{:S(2)}) copy-start(bf16[384,1280]{1,0:T(8,128)(2,1)} %copy-done.6) | copy-start | bytes 2949124
  153.9 8.6 %copy-start.3 = (bf16[384,768]{1,0:T(8,128)(2,1)S(1)}, bf16[384,768]{1,0:T(8,128)(2,1)}, u32[]{:S(2)}) copy-start(bf16[384,768]{1,0:T(8,128)(2,1)} %param.12) | copy-start | bytes 1769476
  153.9 9.5 %copy-start.4 = (bf16[384,512]{1,0:T(8,128)(2,1)S(1)}, bf16[384,512]{1,0:T(8,128)(2,1)}, u32[]{:S(2)}) copy-start(bf16[384,512]{1,0:T(8,128)(2,1)} %param.13) | copy-start | bytes 1179652
  183.2 5.6 %copy-start.1 = (bf16[3,2048,1280]{2,1,0:T(8,128)(2,1)}, bf16[3,2048,1280]{2,1,0:T(8,128)(2,1)S(1)}, u32[]{:S(2)}) copy-start(bf16[3,2048,1280]{2,1,0:T(8,128)(2,1)S(1)} %bitcast_select_fusion) | copy-start | bytes 47185924
  259.3 9.5 %copy-start.12 = (s32[192,1]{0,1:T(1,128)S(1)}, s32[192,1]{0,1:T(1,128)}, u32[]{:S(2)}) copy-start(s32[192,1]{0,1:T(1,128)} %param.17) | copy-start | bytes 2308
  260.3 30.1 %copy-start.13 = (f32[2048]{0:T(1024)S(1)}, f32[2048]{0:T(1024)}, u32[]{:S(2)}) copy-start(f32[2048]{0:T(1024)} %param.16) | copy-start | bytes 24580
  264.2 23.0 %all-to-all-start = ((bf16[2,192,2048]{2,1,0:T(8,128)(2,1)}), bf16[2,192,2048]{2,1,0:T(8,128)(2,1)}, u32[]{:S(2)}, u32[]{:S(2)}) async-start(bf16[2,192,2048]{2,1,0:T(8,128)(2,1)} %bitcast.86), calls=%async_computation | async-start | bytes 3145728 | tf_op jit(solution)/shard_map/all_to_all | solution.py:26
  287.2 20.7 %copy-start.15 = (bf16[1,2048,704]{1,2,0:T(8,128)(2,1)S(1)}, bf16[1,2048,704]{1,2,0:T(8,128)(2,1)}, u32[]{:S(2)}) copy-start(bf16[1,2048,704]{1,2,0:T(8,128)(2,1)} %param.19) | copy-start | bytes 8650756
  289.2 1.2 copy-start.2
  306.8 1.0 copy-start.5
  309.9 19.5 %copy-start.14 = (f32[192,1]{0,1:T(1,128)S(1)}, f32[192,1]{0,1:T(1,128)}, u32[]{:S(2)}) copy-start(f32[192,1]{0,1:T(1,128)} %param.18) | copy-start | bytes 2308
where the time goes:
time: 334 us; the launch traced here: 332 us
  waiting for transfers between devices  143 us (43%)
  local copies, waits for them, and re-layouts  69.7 us (21%)
  matrix products  35.9 us (11%)
  other arithmetic  35.7 us (11%)
  blocking collectives  29.5 us (9%)
  starting transfers between devices  18.2 us (5%)
    ppermute x7, waiting for transfers between devices, shifted(): return lax.ppermute(array, axis, pairs)  126 us
    unnamed x46, local copies, waits for them, and re-layouts  21.3 us
    slice x2, local copies, waits for them, and re-layouts, shards(): picked[:, :, :key_width].reshape(blocks_here, chosen * BLK, heads_here, QK)  20.6 us
    sub x1, other arithmetic, shards(): weights = jnp.exp(scores - row_peak)  17.3 us
    all_to_all x1, waiting for transfers between devices, sum_at_owner(): lax.all_to_all(pieces, axis, split_axis=0, concat_axis=0, tiled=True)  17.2 us
    all_to_all x1, blocking collectives, shards(): lax.all_to_all(outgoing, 'exp', split_axis=0, concat_axis=0, tiled=True)  15.8 us
    all_to_all x1, blocking collectives, shards(): lax.all_to_all(result, 'exp', split_axis=0, concat_axis=0, tiled=True)  13.7 us
    ppermute x7, starting transfers between devices, shifted(): return lax.ppermute(array, axis, pairs)  13.6 us
  transfers between devices with their start and end apart: 8, of which 8 were waited for; matrix products, arithmetic and copies ran while one was open for 3% of the time, Pallas kernels for 0%

commit v1 on v0

v1 whole, which is shorter than its diff:
```python
import functools
import math

import jax
import jax.numpy as jnp
from jax import lax
from jax.experimental import pallas as pl
from jax.experimental.pallas import tpu as pltpu
from jax.sharding import PartitionSpec as P

MESH = pl.DeviceIdType.MESH
F32 = jnp.float32
BF16 = jnp.bfloat16
QK = 192
VD = 128
BLK = 128
TOK = 384
OWN = 192
SPAN = 22
CAP = 144
D = 2048
FF = 704
NCH = 4
WCH = D // NCH
KVR = 960
QR = 608
NEG = -1e30
COEF = QK ** (-0.5) * math.log2(math.e)


def half_turn(a):
    return pltpu.roll(a.astype(F32), 64, 1)


def low_lanes(shape):
    return lax.broadcasted_iota(jnp.int32, shape, 1) < 64


def pack_tail(tile, high):
    a = tile[:OWN].astype(F32)
    b = tile[OWN:].astype(F32)
    if high:
        a = pltpu.roll(a, 64, 1)
    else:
        b = pltpu.roll(b, 64, 1)
    return jnp.where(low_lanes(a.shape), a, b).astype(BF16)


def kernel(
    q_ref, k_ref, v_ref, lay_ref, gain_ref, ids_ref, rw_ref, ow_ref, gw_ref, uw_ref, dw_ref,
    out_ref,
    kst, qst, kv, kt, qraw, qb, bias, m_sc, l_sc, acc, cst, ctx, wb, gwb, uwb, dwb,
    idr, idm, att, nrm, rows, own_res, rst, ret, pm,
    ld, s_kv, r_kv, s_q, r_q, s_f, s_row, s_c, r_c, s_w, r_w, s_id, r_id, s_ret, r_ret,
):
    s = lax.axis_index("seq")
    e = lax.axis_index("exp")
    c = lax.rem(s, 2)
    x = lax.rem(s // 2, 4)
    r = s // 8
    p = lax.rem(s, 8)
    yh = lax.rem(r, 2)
    z = r // 2
    ct = x // 2

    def at(row, xx, cc, ee):
        return (row * 8 + xx * 2 + cc, ee)

    nxt = lax.rem(r + 1, 16)
    prv = lax.rem(r + 15, 16)
    cross = (z * 2 + (1 - yh)) * 8 + p
    up = (s + e * (cross - s), 1 - e)
    down = (cross + e * (s - cross), 1 - e)

    loads = [
        pltpu.make_async_copy(ow_ref, wb.at[e], ld.at[0]),
        pltpu.make_async_copy(gw_ref, gwb, ld.at[1]),
        pltpu.make_async_copy(uw_ref, uwb, ld.at[2]),
        pltpu.make_async_copy(dw_ref, dwb, ld.at[3]),
    ]
    for one in loads:
        one.start()

    bar = pltpu.get_barrier_semaphore()
    for dp in range(8):
        for de in range(2):
            if dp or de:
                who = (r * 8 + lax.rem(p + dp, 8), lax.rem(e + de, 2))
                pl.semaphore_signal(bar, inc=1, device_id=who, device_id_type=MESH)
    for row in (nxt, prv):
        for cc in range(2):
            pl.semaphore_signal(bar, inc=1, device_id=at(row, x, cc, e), device_id_type=MESH)
    pl.semaphore_signal(bar, inc=1, device_id=(cross, 1 - e), device_id_type=MESH)

    for h in range(4):
        main = (0, 2, 3, 5)[h]
        tail = (1, 1, 4, 4)[h]
        high = h % 2 == 1
        kst[h, 0:384] = k_ref[:, main * 128 : main * 128 + 128]
        kst[h, 384:576] = pack_tail(k_ref[:, tail * 128 : tail * 128 + 128], high)
        kst[h, 576:960] = v_ref[:, h * 128 : h * 128 + 128]
        qst[h, 0:384] = q_ref[:, main * 128 : main * 128 + 128]
        qst[h, 384:576] = pack_tail(q_ref[:, tail * 128 : tail * 128 + 128], high)
    row_i = lax.broadcasted_iota(jnp.int32, (32, 128), 0)
    lane_i = lax.broadcasted_iota(jnp.int32, (32, 128), 1)
    jq = lax.rem(row_i, 3)
    win = (row_i // 3) * 3 + lane_i
    off = SPAN - 1 + jq - win
    seen = jnp.zeros((32, 128), jnp.bool_)
    for t in range(16):
        mine = jnp.where(jq == 0, lay_ref[0, t], jnp.where(jq == 1, lay_ref[1, t], lay_ref[2, t]))
        seen = seen | (off == mine)
    seen = seen & (off >= 0) & (3 * s - (SPAN - 1) + win >= 0)
    mask = jnp.where(seen, 0.0, NEG).astype(BF16)
    for h in range(4):
        qst[h, 576:608] = mask
    col = jnp.broadcast_to(ids_ref[...].astype(F32), (OWN, 128))
    col = jnp.concatenate([col, jnp.full((64, 128), 5.0, F32)], axis=0)
    idm[...] = jnp.transpose(col)[0:8]

    pl.semaphore_wait(bar, 20)

    w_out = []
    for d, who in ((0, up), (1, down)):
        quarter = pl.multiple_of((2 * c + d) * 128, 128)
        one = pltpu.make_async_remote_copy(
            src_ref=ow_ref.at[pl.ds(quarter, 128)],
            dst_ref=wb.at[e, pl.ds(quarter, 128)],
            send_sem=s_w.at[d],
            recv_sem=r_w.at[2 * c + d],
            device_id=who,
            device_id_type=MESH,
        )
        one.start()
        w_out.append(one)
    send_id = pltpu.make_async_remote_copy(
        src_ref=idm, dst_ref=idr, send_sem=s_id, recv_sem=r_id, device_id=(s, 1 - e), device_id_type=MESH
    )
    send_id.start()

    def kv_copy(d):
        xx = lax.rem(x + d, 4)
        return pltpu.make_async_remote_copy(
            src_ref=kst.at[xx], dst_ref=kv.at[8 + p], send_sem=s_kv.at[d], recv_sem=r_kv.at[8 + p],
            device_id=at(r, xx, ct, e), device_id_type=MESH,
        )

    def q_copy(d):
        xx = lax.rem(x + d, 4)
        return pltpu.make_async_remote_copy(
            src_ref=qst.at[xx], dst_ref=qraw.at[lax.rem(p, 4)], send_sem=s_q.at[d], recv_sem=r_q.at[lax.rem(p, 4)],
            device_id=at(r, xx, ct, e), device_id_type=MESH,
        )

    for copy_of in (kv_copy, q_copy):
        for d in (1, 3, 2):
            copy_of(d).start()

        @pl.when(c != ct)
        def _():
            copy_of(0).start()

    @pl.when(c == ct)
    def _():
        kv[8 + p] = kst[x]
        qraw[lax.rem(p, 4)] = qst[x]

    def kv_wait(slot):
        pltpu.make_async_remote_copy(
            src_ref=kst.at[0], dst_ref=kv.at[slot], send_sem=s_kv.at[0], recv_sem=r_kv.at[slot],
            device_id=at(r, x, 1 - c, e), device_id_type=MESH,
        ).wait_recv()

    def to_core1(slot):
        return pltpu.make_async_remote_copy(
            src_ref=kv.at[slot], dst_ref=kv.at[slot], send_sem=s_f.at[slot], recv_sem=r_kv.at[slot],
            device_id=at(r, x, 1, e), device_id_type=MESH,
        )

    def to_next(slot):
        return pltpu.make_async_remote_copy(
            src_ref=kv.at[slot], dst_ref=kv.at[slot - 8], send_sem=s_row.at[slot - 8], recv_sem=r_kv.at[slot - 8],
            device_id=at(nxt, x, 0, e), device_id_type=MESH,
        )

    def unpack(slot):
        t = kv[slot, 384:576]
        kt[slot, 0:192] = t
        kt[slot, 192:384] = half_turn(t).astype(BF16)

    def clear(g, carry):
        m_sc[g] = jnp.full((TOK, 128), -3e38, F32)
        l_sc[g] = jnp.zeros((TOK, 128), F32)
        acc[g] = jnp.zeros((TOK, 128), F32)
        return carry

    lax.fori_loop(0, 4, clear, 0)

    def arrive(i, carry):
        slot = 8 + 4 * c + lax.rem(2 * lax.rem(x, 2) + 2 * (1 - lax.rem(x, 2)) * 0 + i, 4)

        @pl.when(slot != 8 + p)
        def _():
            kv_wait(slot)

        @pl.when(slot > 8)
        def _():
            to_next(slot).start()

        @pl.when(c == 0)
        def _():
            to_core1(slot).start()

        unpack(slot)
        return carry

    lax.fori_loop(0, 4, arrive, 0)

    def take_q(g, carry):
        @pl.when(4 * c + g != p)
        def _():
            pltpu.make_async_remote_copy(
                src_ref=qst.at[0], dst_ref=qraw.at[g], send_sem=s_q.at[0], recv_sem=r_q.at[g],
                device_id=at(r, x, 1 - c, e), device_id_type=MESH,
            ).wait_recv()

        qb[g, :, 0:128] = qraw[g, 0:384]
        t = qraw[g, 384:576].astype(F32)
        low = low_lanes(t.shape)
        qb[g, 0:192, 128:256] = jnp.where(low, t, 0.0).astype(BF16)
        qb[g, 192:384, 128:256] = jnp.where(low, half_turn(t), 0.0).astype(BF16)
        b = qraw[g, 576:608].astype(F32)
        for j in range(3):
            bias[g, :, j * 128 : j * 128 + 128] = jnp.broadcast_to(b[:, j : j + 1], (32, 128))
        return carry

    lax.fori_loop(0, 4, take_q, 0)

    def tile(g, slot, diag):
        keys = jnp.concatenate([kv[slot, 0:384], kt[slot]], axis=1)
        vals = kv[slot, 576:960]
        sc = lax.dot_general(qb[g], keys, (((1,), (1,)), ((), ())), preferred_element_type=F32)
        k = slot - (4 * c + g) - 1
        for j in range(3):
            own = slice(j * 128, j * 128 + 128)
            sj = sc[own] + bias[g, pl.ds(3 * k + j, 1), :]
            if diag:
                qi = lax.broadcasted_iota(jnp.int32, (128, TOK), 0) + j * 128
                ki = lax.broadcasted_iota(jnp.int32, (128, TOK), 1)
                sj = jnp.where(ki <= qi, sj, NEG)
            top = jnp.maximum(jnp.maximum(sj[:, 0:128], sj[:, 128:256]), sj[:, 256:384])
            m_old = m_sc[g, own]
            m_new = jnp.maximum(m_old, jnp.max(top, axis=1, keepdims=True))
            fade = jnp.exp2((m_old - m_new) * COEF)
            parts = [jnp.exp2((sj[:, i * 128 : i * 128 + 128] - m_new) * COEF) for i in range(3)]
            m_sc[g, own] = m_new
            l_sc[g, own] = l_sc[g, own] * fade + (parts[0] + parts[1] + parts[2])
            pr = jnp.concatenate([a.astype(BF16) for a in parts], axis=1)
            acc[g, own] = acc[g, own] * fade + jnp.dot(pr, vals, preferred_element_type=F32)

    def own_row(i, carry):
        slot = 8 + i

        @pl.when((c == 1) & (i < 4))
        def _():
            kv_wait(slot)
            unpack(slot)

        first = i - 4 * c

        @pl.when(first >= 0)
        def _():
            tile(first, slot, True)

        def inner(g, carry2):
            tile(g, slot, False)
            return carry2

        lax.fori_loop(jnp.maximum(first + 1, 0), 4, inner, 0)
        return carry

    lax.fori_loop(0, 4 + 4 * c, own_row, 0)

    def prev_row(i, carry):
        half = i // 2
        odd = i - 2 * half
        slot = (1 - c) * (7 - 4 * odd - half) + c * (7 - i)
        kv_wait(slot)

        @pl.when((c == 0) & (slot >= 5))
        def _():
            to_core1(slot).start()

        unpack(slot)

        def inner(g, carry2):
            tile(g, slot, False)
            return carry2

        lax.fori_loop(0, jnp.minimum(slot - 4 * c, 4), inner, 0)
        return carry

    lax.fori_loop(0, 7 - 4 * c, prev_row, 0)

    head = 4 * e + x

    def ctx_copy(g, de):
        return pltpu.make_async_remote_copy(
            src_ref=cst.at[g], dst_ref=ctx.at[head], send_sem=s_c.at[2 * g + de], recv_sem=r_c.at[head],
            device_id=at(r, 2 * c + g // 2, lax.rem(g, 2), lax.rem(e + de, 2)), device_id_type=MESH,
        )

    def finish(g, carry):
        total = jnp.sum(l_sc[g], axis=1, keepdims=True)
        cst[g] = (acc[g] / total).astype(BF16)
        ctx_copy(g, 1).start()

        @pl.when(4 * c + g != p)
        def _():
            ctx_copy(g, 0).start()

        @pl.when(4 * c + g == p)
        def _():
            ctx[head] = cst[g]

        return carry

    lax.fori_loop(0, 4, finish, 0)

    def w_copy(quarter):
        start = pl.multiple_of(quarter * 128, 128)
        return pltpu.make_async_remote_copy(
            src_ref=wb.at[1 - e, pl.ds(start, 128)], dst_ref=wb.at[1 - e, pl.ds(start, 128)],
            send_sem=s_w.at[2 + lax.rem(quarter, 2)], recv_sem=r_w.at[quarter],
            device_id=at(r, x, 1 - c, e), device_id_type=MESH,
        )

    for d in range(2):
        w_copy(2 * c + d).wait_recv()
        w_copy(2 * c + d).start()

    send_id.wait_recv()
    upper = (
        lax.broadcasted_iota(jnp.int32, (256, 256), 0) <= lax.broadcasted_iota(jnp.int32, (256, 256), 1)
    ).astype(BF16)
    for n, (src, who) in enumerate(((idr, e), (idm, e), (idm, 1 - e))):
        member = (src[...] == who.astype(F32)).astype(F32)
        member = jnp.concatenate([member, member], axis=0)
        rank = jnp.dot(member.astype(BF16), upper, preferred_element_type=F32)
        rank = jnp.where(member > 0.5, rank - 1.0, -1.0)[0:1]
        slots = lax.broadcasted_iota(jnp.int32, (CAP, 256), 0).astype(F32)
        pm[n] = jnp.where(slots == rank, 1.0, 0.0).astype(BF16)

    for one in loads:
        one.wait()
    for d in range(2):
        w_copy(2 * (1 - c) + d).wait_recv()

    def ctx_wait(h, carry):
        @pl.when((h != head) | (c != ct))
        def _():
            pltpu.make_async_remote_copy(
                src_ref=cst.at[0], dst_ref=ctx.at[h], send_sem=s_c.at[0], recv_sem=r_c.at[h],
                device_id=at(r, x, 1 - c, e), device_id_type=MESH,
            ).wait_recv()

        return carry

    lax.fori_loop(0, 8, ctx_wait, 0)

    def project(n, carry):
        cols = pl.ds(pl.multiple_of(n * WCH, WCH), WCH)
        total = jnp.zeros((TOK, WCH), F32)
        for side in range(2):
            left = jnp.concatenate([ctx[4 * side + i] for i in range(4)], axis=1)
            total = total + jnp.dot(left, wb[side, :, cols], preferred_element_type=F32)
        att[:, cols] = total
        sq = total * total
        part = sq[:, 0:128]
        for i in range(1, WCH // 128):
            part = part + sq[:, i * 128 : i * 128 + 128]
        return carry + part

    sums = lax.fori_loop(0, NCH, project, jnp.zeros((TOK, 128), F32))
    scale = lax.rsqrt(jnp.sum(sums, axis=1, keepdims=True) * (1.0 / D) + 1e-06)

    def normalize(n, carry):
        cols = pl.ds(pl.multiple_of(n * WCH, WCH), WCH)
        val = (att[:, cols] * scale * gain_ref[:, cols]).astype(BF16)
        for side in range(2):
            nrm[side, 0:OWN, cols] = val[side * OWN : side * OWN + OWN]
            nrm[side, OWN:256, cols] = jnp.zeros((64, WCH), BF16)
        rows[0:CAP, cols] = jnp.dot(pm[0], nrm[1 - e, :, cols], preferred_element_type=F32).astype(BF16)
        rows[CAP : 2 * CAP, cols] = jnp.dot(pm[1], nrm[e, :, cols], preferred_element_type=F32).astype(BF16)
        return carry

    lax.fori_loop(0, NCH, normalize, 0)

    gate = jnp.dot(rows[...], gwb[...], preferred_element_type=F32)
    upp = jnp.dot(rows[...], uwb[...], preferred_element_type=F32)
    hidden = (gate * jax.nn.sigmoid(gate) * upp).astype(BF16)

    def ret_copy(n):
        return pltpu.make_async_remote_copy(
            src_ref=rst.at[n], dst_ref=ret.at[n], send_sem=s_ret.at[n], recv_sem=r_ret.at[n],
            device_id=(s, 1 - e), device_id_type=MESH,
        )

    for n in range(NCH):
        cols = slice(n * WCH, n * WCH + WCH)
        res = jnp.dot(hidden, dwb[:, cols], preferred_element_type=F32).astype(BF16)
        rst[n] = res[0:CAP]
        own_res[n] = res[CAP : 2 * CAP]
        ret_copy(n).start()

    for n in range(NCH):
        cols = slice(n * WCH, n * WCH + WCH)
        got = lax.dot_general(pm[1], own_res[n], (((0,), (0,)), ((), ())), preferred_element_type=F32)
        ret_copy(n).wait_recv()
        got = got + lax.dot_general(pm[2], ret[n], (((0,), (0,)), ((), ())), preferred_element_type=F32)
        base = att[pl.ds(pl.multiple_of(e * OWN, OWN), OWN), cols]
        out_ref[:, cols] = (base + rw_ref[...] * got[0:OWN]).astype(BF16)

    for n in range(NCH):
        ret_copy(n).wait_send()
    for d in (1, 2, 3):
        kv_copy(d).wait_send()
        q_copy(d).wait_send()

    @pl.when(c != ct)
    def _():
        kv_copy(0).wait_send()
        q_copy(0).wait_send()

    def sent(i, carry):
        slot = 8 + 4 * c + i

        @pl.when(slot > 8)
        def _():
            to_next(slot).wait_send()

        @pl.when(c == 0)
        def _():
            to_core1(slot).wait_send()

        return carry

    lax.fori_loop(0, 4, sent, 0)

    def sent_prev(i, carry):
        to_core1(5 + i).wait_send()
        return carry

    lax.fori_loop(0, 3 - 3 * c, sent_prev, 0)

    def sent_ctx(g, carry):
        ctx_copy(g, 1).wait_send()

        @pl.when(4 * c + g != p)
        def _():
            ctx_copy(g, 0).wait_send()

        return carry

    lax.fori_loop(0, 4, sent_ctx, 0)
    for one in w_out:
        one.wait_send()
    for d in range(2):
        w_copy(2 * c + d).wait_send()
    send_id.wait_send()


def shards(
    queries, key_heads, value_heads, block_layout, out_weight, norm_gain, expert_ids, route_weight,
    gate_weight, up_weight, down_weight,
):
    vm = pl.BlockSpec(memory_space=pltpu.VMEM)
    anyspace = pl.BlockSpec(memory_space=pl.ANY)
    dma = pltpu.SemaphoreType.DMA
    return pl.pallas_call(
        kernel,
        out_shape=jax.ShapeDtypeStruct((OWN, D), BF16),
        in_specs=[vm, vm, vm, pl.BlockSpec(memory_space=pltpu.SMEM), vm, vm, vm] + [anyspace] * 4,
        out_specs=vm,
        scratch_shapes=[
            pltpu.VMEM((4, KVR, 128), BF16),
            pltpu.VMEM((4, QR, 128), BF16),
            pltpu.VMEM((16, KVR, 128), BF16),
            pltpu.VMEM((16, TOK, 128), BF16),
            pltpu.VMEM((4, QR, 128), BF16),
            pltpu.VMEM((4, TOK, 256), BF16),
            pltpu.VMEM((4, 32, TOK), F32),
            pltpu.VMEM((4, TOK, 128), F32),
            pltpu.VMEM((4, TOK, 128), F32),
            pltpu.VMEM((4, TOK, 128), F32),
            pltpu.VMEM((4, TOK, 128), BF16),
            pltpu.VMEM((8, TOK, 128), BF16),
            pltpu.VMEM((2, 512, D), BF16),
            pltpu.VMEM((D, FF), BF16),
            pltpu.VMEM((D, FF), BF16),
            pltpu.VMEM((FF, D), BF16),
            pltpu.VMEM((8, 256), F32),
            pltpu.VMEM((8, 256), F32),
            pltpu.VMEM((TOK, D), F32),
            pltpu.VMEM((2, 256, D), BF16),
            pltpu.VMEM((2 * CAP, D), BF16),
            pltpu.VMEM((NCH, CAP, WCH), BF16),
            pltpu.VMEM((NCH, CAP, WCH), BF16),
            pltpu.VMEM((NCH, CAP, WCH), BF16),
            pltpu.VMEM((3, CAP, 256), BF16),
            dma((4,)),
            dma((4,)), dma((16,)),
            dma((4,)), dma((4,)),
            dma((16,)), dma((8,)),
            dma((8,)), dma((8,)),
            dma((4,)), dma((4,)),
            dma, dma,
            dma((NCH,)), dma((NCH,)),
        ],
        compiler_params=pltpu.CompilerParams(
            collective_id=0, has_side_effects=True, vmem_limit_bytes=60 * 1024 * 1024
        ),
        name="layer",
    )(
        queries, key_heads, value_heads, block_layout, norm_gain.reshape(1, D), expert_ids, route_weight,
        out_weight, gate_weight[0], up_weight[0], down_weight[0],
    )


def solution(mesh):
    in_specs = (
        P("seq", "exp"),
        P("seq", "exp"),
        P("seq", "exp"),
        P("seq", None),
        P("exp", None),
        P(),
        P(("seq", "exp"), None),
        P(("seq", "exp"), None),
        P("exp", None, None),
        P("exp", None, None),
        P("exp", None, None),
    )
    out_specs = P(("seq", "exp"), None)
    return jax.shard_map(shards, mesh=mesh, in_specs=in_specs, out_specs=out_specs, check_vma=False)
```

time: 334 us -> 98 us (0.29)
  the two profiles are of different devices: /device:TPU:128 before, /device:TPU:17 now
where the time goes in v1:
time: 98 us; the launch traced here: 97.8 us
  Pallas kernels  85.3 us (87%)
  local copies, waits for them, and re-layouts  12.5 us (13%)
    pallas_call x1, Pallas kernels, shards(): pl.pallas_call(kernel, out_shape=jax.ShapeDtypeStruct((OWN, D), BF16), in...  85.3 us
    unnamed x7, local copies, waits for them, and re-layouts  12.5 us

profile of v1, /device:TPU:17, one launch (start us, length us, event | category | flops | bytes accessed | tf_op | source)
XLA Modules:
  0.0 97.8 jit_solution(16805848404985101356)
XLA Ops:
  0.0 1.4 %copy.14.ids_ref = s32[192,1]{1,0:T(8,128)} copy(s32[192,1]{0,1:T(1,128)} %param.17) | data formatting | bytes 1536 | tf_op args[6]
  1.4 1.4 %copy.15.rw_ref = f32[192,1]{1,0:T(8,128)} copy(f32[192,1]{0,1:T(1,128)} %param.18) | data formatting | bytes 1536 | tf_op args[7]
  2.9 0.0 copy-start
  2.9 4.7 %copy.12 = bf16[1,2048,704]{2,1,0:T(8,128)(2,1)} copy(bf16[1,2048,704]{1,2,0:T(8,128)(2,1)} %param.19) | data formatting | bytes 5767168 | tf_op args[8]
  7.6 0.0 copy-done
  7.6 2.8 %copy.13 = bf16[1,2048,704]{2,1,0:T(8,128)(2,1)} copy(bf16[1,2048,704]{1,2,0:T(8,128)(2,1)S(1)} %copy-done) | data formatting | bytes 5767168 | tf_op args[9]
  10.5 85.3 %layer.1 = bf16[192,2048]{1,0:T(8,128)(2,1)} custom-call(bf16[384,768]{1,0:T(8,128)(2,1)} %q_ref.1, bf16[384,768]{1,0:T(8,128)(2,1)} %k_ref.1, bf16[384,512]{1,0:T(8,128)(2,1)} %v_ref.1, s32[3,16]{1,0:T(4,128)} %lay_ref.1, f32[1,2048]{1,0:T(1,128)} %bitcast.7, s32[192,1]{1,0:T(8,128)} %copy.14.ids_ref, f32[192,1]{1,0:T(8,128)} %copy.15.rw_ref, ...), custom_call_target="tpu_custom_call" | custom-call | tf_op jit(solution)/shard_map/layer/pallas_call | solution.py:480
  95.7 2.1 %copy.17 = bf16[192,2048]{1,0:T(8,128)(2,1)} copy(bf16[192,2048]{1,0:T(8,128)(2,1)} %layer.1) | data formatting | bytes 1572864
Async XLA Ops:
  2.9 4.8 %copy-start = (bf16[1,2048,704]{1,2,0:T(8,128)(2,1)S(1)}, bf16[1,2048,704]{1,2,0:T(8,128)(2,1)}, u32[]{:S(2)}) copy-start(bf16[1,2048,704]{1,2,0:T(8,128)(2,1)} %param.20) | copy-start | bytes 8650756

commit v2 on v1

v2 whole, which is shorter than its diff:
```python
import functools
import math

import jax
import jax.numpy as jnp
from jax import lax
from jax.experimental import pallas as pl
from jax.experimental.pallas import tpu as pltpu
from jax.sharding import PartitionSpec as P

MESH = pl.DeviceIdType.MESH
F32 = jnp.float32
BF16 = jnp.bfloat16
QK = 192
VD = 128
BLK = 128
TOK = 384
OWN = 192
SPAN = 22
CAP = 144
D = 2048
FF = 704
NCH = 4
WCH = D // NCH
PAIR = 768
KVR = 960
QR = 736
NEG = -1e30
COEF = QK ** (-0.5) * math.log2(math.e)


def half_turn(a):
    return pltpu.roll(a.astype(F32), 64, 1)


def turned(a):
    return jnp.transpose(a.astype(F32)).astype(BF16)


def low_lanes(shape):
    return lax.broadcasted_iota(jnp.int32, shape, 1) < 64


def pack_tail(tile, high):
    a = tile[:OWN].astype(F32)
    b = tile[OWN:].astype(F32)
    if high:
        a = pltpu.roll(a, 64, 1)
    else:
        b = pltpu.roll(b, 64, 1)
    return jnp.where(low_lanes(a.shape), a, b).astype(BF16)


def kernel(
    q_hbm, k_hbm, v_hbm, lay_ref, gain_ref, ids_ref, rw_ref, ow_ref, gw_ref, uw_ref, dw_ref,
    out_ref,
    q_ref, k_ref, v_ref, kst, qst, kv, kt, qraw, qb, bias, m_sc, l_sc, acc, sa, sb, pa, pb, cst, ctx, wb, gwb, uwb, dwb,
    idr, idm, rwr, rwc, att, nrm, rows, own_res, rst, ret, pm,
    ld, s_kv, r_kv, s_q, r_q, s_f, s_row, s_c, r_c, s_w, r_w, s_id, r_id, s_ret, r_ret,
):
    s = lax.axis_index("seq")
    e = lax.axis_index("exp")
    c = lax.rem(s, 2)
    x = lax.rem(s // 2, 4)
    r = s // 8
    p = lax.rem(s, 8)
    yh = lax.rem(r, 2)
    z = r // 2
    ct = x // 2

    def at(row, xx, cc, ee):
        return (row * 8 + xx * 2 + cc, ee)

    nxt = lax.rem(r + 1, 16)
    prv = lax.rem(r + 15, 16)
    cross = (z * 2 + (1 - yh)) * 8 + p
    up = (s + e * (cross - s), 1 - e)
    down = (cross + e * (s - cross), 1 - e)

    bar = pltpu.get_barrier_semaphore()
    for dp in range(8):
        for de in range(2):
            if dp or de:
                who = (r * 8 + lax.rem(p + dp, 8), lax.rem(e + de, 2))
                pl.semaphore_signal(bar, inc=1, device_id=who, device_id_type=MESH)
    for row in (nxt, prv):
        for cc in range(2):
            pl.semaphore_signal(bar, inc=1, device_id=at(row, x, cc, e), device_id_type=MESH)
    pl.semaphore_signal(bar, inc=1, device_id=(cross, 1 - e), device_id_type=MESH)

    load_k = pltpu.make_async_copy(k_hbm, k_ref, ld.at[4])
    load_v = pltpu.make_async_copy(v_hbm, v_ref, ld.at[5])
    load_q = pltpu.make_async_copy(q_hbm, q_ref, ld.at[6])
    loads = [
        pltpu.make_async_copy(ow_ref, wb.at[e], ld.at[0]),
        pltpu.make_async_copy(gw_ref, gwb, ld.at[1]),
        pltpu.make_async_copy(uw_ref, uwb, ld.at[2]),
        pltpu.make_async_copy(dw_ref, dwb, ld.at[3]),
    ]
    for one in [load_k, load_v, load_q] + loads:
        one.start()

    load_k.wait()
    load_v.wait()
    for h in range(4):
        main = (0, 2, 3, 5)[h]
        tail = (1, 1, 4, 4)[h]
        kst[h, 0:384] = k_ref[:, main * 128 : main * 128 + 128]
        kst[h, 384:576] = pack_tail(k_ref[:, tail * 128 : tail * 128 + 128], h % 2 == 1)
        for j in range(3):
            kst[h, 576 + j * 128 : 704 + j * 128] = turned(v_ref[j * 128 : j * 128 + 128, h * 128 : h * 128 + 128])

    pl.semaphore_wait(bar, 20)

    def kv_copy(d):
        xx = lax.rem(x + d, 4)
        return pltpu.make_async_remote_copy(
            src_ref=kst.at[xx], dst_ref=kv.at[8 + p], send_sem=s_kv.at[d], recv_sem=r_kv.at[8 + p],
            device_id=at(r, xx, ct, e), device_id_type=MESH,
        )

    def q_copy(d):
        xx = lax.rem(x + d, 4)
        return pltpu.make_async_remote_copy(
            src_ref=qst.at[xx], dst_ref=qraw.at[lax.rem(p, 4)], send_sem=s_q.at[d], recv_sem=r_q.at[lax.rem(p, 4)],
            device_id=at(r, xx, ct, e), device_id_type=MESH,
        )

    def spread(copy_of):
        for d in (1, 3, 2):
            copy_of(d).start()

        @pl.when(c != ct)
        def _():
            copy_of(0).start()

    spread(kv_copy)

    load_q.wait()
    for j in range(3):
        for t in range(6):
            piece = turned(q_ref[j * 128 : j * 128 + 128, t * 128 : t * 128 + 128])
            if t in (0, 2, 3, 5):
                h = {0: 0, 2: 1, 3: 2, 5: 3}[t]
                qst[h, j * 192 : j * 192 + 128] = piece
            else:
                h = {1: 0, 4: 2}[t]
                qst[h, j * 192 + 128 : j * 192 + 192] = piece[0:64]
                qst[h + 1, j * 192 + 128 : j * 192 + 192] = piece[64:128]
    row_i = lax.broadcasted_iota(jnp.int32, (160, 128), 0)
    jq = lax.broadcasted_iota(jnp.int32, (160, 128), 1)
    jk = lax.rem(row_i, 16)
    win = 3 * (row_i // 16 - 1) + jk
    off = SPAN - 1 + jq - win
    seen = jnp.zeros((160, 128), jnp.bool_)
    for t in range(16):
        mine = jnp.where(jq == 0, lay_ref[0, t], jnp.where(jq == 1, lay_ref[1, t], lay_ref[2, t]))
        seen = seen | (off == mine)
    seen = seen & (off >= 0) & (3 * s - (SPAN - 1) + win >= 0)
    mask = jnp.where(seen | (jk >= 3), 0.0, NEG).astype(BF16)
    for h in range(4):
        qst[h, 576:736] = mask
    spread(q_copy)

    idm[...] = jnp.full((8, 256), 5.0, F32)
    idm[:, 0:OWN] = jnp.broadcast_to(ids_ref[...].astype(F32), (8, OWN))
    rwr[...] = jnp.zeros((8, 256), F32)
    rwr[:, 0:OWN] = jnp.broadcast_to(rw_ref[...], (8, OWN))
    rwc[...] = jnp.transpose(jnp.broadcast_to(rwr[0:1], (128, 256)))[0:OWN]
    send_id = pltpu.make_async_remote_copy(
        src_ref=idm, dst_ref=idr, send_sem=s_id, recv_sem=r_id, device_id=(s, 1 - e), device_id_type=MESH
    )
    send_id.start()

    @pl.when(c == ct)
    def _():
        kv[8 + p] = kst[x]
        qraw[lax.rem(p, 4)] = qst[x]

    def kv_wait(slot):
        pltpu.make_async_remote_copy(
            src_ref=kst.at[0], dst_ref=kv.at[slot], send_sem=s_kv.at[0], recv_sem=r_kv.at[slot],
            device_id=at(r, x, 1 - c, e), device_id_type=MESH,
        ).wait_recv()

    def to_core1(slot):
        return pltpu.make_async_remote_copy(
            src_ref=kv.at[slot], dst_ref=kv.at[slot], send_sem=s_f.at[slot], recv_sem=r_kv.at[slot],
            device_id=at(r, x, 1, e), device_id_type=MESH,
        )

    def to_next(slot):
        return pltpu.make_async_remote_copy(
            src_ref=kv.at[slot], dst_ref=kv.at[slot - 8], send_sem=s_row.at[slot - 8], recv_sem=r_kv.at[slot - 8],
            device_id=at(nxt, x, 0, e), device_id_type=MESH,
        )

    def unpack(slot):
        t = kv[slot, 384:576].astype(F32)
        for part, val in ((0, t), (1, pltpu.roll(t, 64, 1))):
            lane = lax.broadcasted_iota(jnp.int32, val.shape, 1)
            block = (lax.broadcasted_iota(jnp.int32, val.shape, 0) + part * OWN) // 128
            mark = jnp.where(lane == 64 + block, 1.0, 0.0)
            kt[slot, part * OWN : part * OWN + OWN] = jnp.where(lane < 64, val, mark).astype(BF16)

    m_sc[...] = jnp.full((2, 8, PAIR), -3e38, F32)
    l_sc[...] = jnp.zeros((2, 8, PAIR), F32)
    acc[...] = jnp.zeros((2, 128, PAIR), F32)
    bias[...] = jnp.full((2, 12, 16, PAIR), NEG, BF16)
    qb[...] = jnp.zeros((2, 256, PAIR), BF16)

    def arrive(i, carry):
        slot = 8 + 4 * c + lax.rem(2 * lax.rem(x, 2) + i, 4)

        @pl.when(slot != 8 + p)
        def _():
            kv_wait(slot)

        @pl.when(slot > 8)
        def _():
            to_next(slot).start()

        @pl.when(c == 0)
        def _():
            to_core1(slot).start()

        unpack(slot)
        return carry

    lax.fori_loop(0, 4, arrive, 0)

    w_out = []
    for d, who in ((0, up), (1, down)):
        quarter = pl.multiple_of((2 * c + d) * 128, 128)
        one = pltpu.make_async_remote_copy(
            src_ref=ow_ref.at[pl.ds(quarter, 128)],
            dst_ref=wb.at[e, pl.ds(quarter, 128)],
            send_sem=s_w.at[d],
            recv_sem=r_w.at[2 * c + d],
            device_id=who,
            device_id_type=MESH,
        )
        one.start()
        w_out.append(one)

    for g in range(4):

        @pl.when(4 * c + g != p)
        def _():
            pltpu.make_async_remote_copy(
                src_ref=qst.at[0], dst_ref=qraw.at[g], send_sem=s_q.at[0], recv_sem=r_q.at[g],
                device_id=at(r, x, 1 - c, e), device_id_type=MESH,
            ).wait_recv()

        odd = g % 2
        for j in range(3):
            cols = slice(odd * TOK + j * 128, odd * TOK + j * 128 + 128)
            qb[g // 2, 0:192, cols] = qraw[g, j * 192 : j * 192 + 192]
            for k in range(10):
                b = qraw[g, 576 + 16 * k : 592 + 16 * k].astype(F32)
                bias[g // 2, k + odd, :, cols] = jnp.broadcast_to(b[:, j : j + 1], (16, 128)).astype(BF16)

    score_buf = (sa, sb)
    prob_buf = (pa, pb)

    def tiles(work):
        chunks = [(pair, slot, diag, n) for pair, slot, diag in work for n in range(PAIR // 256)]
        fades = [None] * len(chunks)

        def scores(i):
            pair, slot, diag, n = chunks[i]
            if n == 0:
                qb[pair, 192:208] = bias[pair, slot - (4 * c + 2 * pair)]
            keys = jnp.concatenate([kv[slot, 0:384], kt[slot]], axis=1)
            score_buf[i % 2][...] = jnp.dot(
                keys, qb[pair, :, n * 256 : n * 256 + 256], preferred_element_type=F32
            )

        def probabilities(i):
            pair, slot, diag, n = chunks[i]
            cols = slice(n * 256, n * 256 + 256)
            parts = []
            for j in range(3):
                sj = score_buf[i % 2][j * 128 : j * 128 + 128]
                if diag:
                    ki = lax.broadcasted_iota(jnp.int32, (128, 256), 0) + j * 128
                    qi = lax.broadcasted_iota(jnp.int32, (128, 256), 1) + n * 256
                    sj = jnp.where(ki <= qi + TOK * (8 + 4 * c + 2 * pair - slot), sj, NEG)
                parts.append(sj)
            top = jnp.max(jnp.maximum(jnp.maximum(parts[0], parts[1]), parts[2]), axis=0, keepdims=True)
            m_old = m_sc[pair, 0:1, cols]
            m_new = jnp.maximum(m_old, top)
            fades[i] = jnp.exp2((m_old - m_new) * COEF)
            m_sc[pair, :, cols] = jnp.broadcast_to(m_new, (8, 256))
            mass = jnp.zeros((8, 256), F32)
            for j in range(3):
                pj = jnp.exp2((parts[j] - m_new) * COEF)
                mass = mass + jnp.sum(pj.reshape(16, 8, 256), axis=0)
                prob_buf[i % 2][j * 128 : j * 128 + 128] = pj.astype(BF16)
            l_sc[pair, :, cols] = l_sc[pair, :, cols] * fades[i] + mass

        def context(i):
            pair, slot, diag, n = chunks[i]
            cols = slice(n * 256, n * 256 + 256)
            vals = jnp.concatenate([kv[slot, 576 + j * 128 : 704 + j * 128] for j in range(3)], axis=1)
            acc[pair, :, cols] = acc[pair, :, cols] * fades[i] + jnp.dot(
                vals, prob_buf[i % 2][...], preferred_element_type=F32
            )

        for t in range(len(chunks) + 2):
            if t < len(chunks):
                scores(t)
            if 0 <= t - 1 < len(chunks):
                probabilities(t - 1)
            if t >= 2:
                context(t - 2)

    def early(i, carry):
        slot = 8 + i
        kv_wait(slot)
        unpack(slot)
        tiles([(0, slot, False), (1, slot, False)])
        return carry

    lax.fori_loop(0, 4 * c, early, 0)

    base = 8 + 4 * c
    tiles(
        [
            (0, base, True),
            (1, base, False),
            (0, base + 1, True),
            (1, base + 1, False),
            (1, base + 2, True),
            (1, base + 3, True),
        ]
    )

    def prev_row(i, carry):
        half = i // 2
        odd = i - 2 * half
        slot = (1 - c) * (7 - 4 * odd - half) + c * (7 - i)
        kv_wait(slot)

        @pl.when((c == 0) & (slot >= 5))
        def _():
            to_core1(slot).start()

        unpack(slot)

        @pl.when(slot >= 4 * c + 3)
        def _():
            tiles([(0, slot, False), (1, slot, False)])

        @pl.when(slot < 4 * c + 3)
        def _():
            tiles([(0, slot, False)])

        return carry

    lax.fori_loop(0, 7 - 4 * c, prev_row, 0)

    head = 4 * e + x

    def ctx_copy(g, de, kind):
        to_e = lax.rem(e + de, 2)
        side = kind * to_e + (1 - kind) * (1 - to_e)
        return pltpu.make_async_remote_copy(
            src_ref=cst.at[g, side], dst_ref=ctx.at[kind, head],
            send_sem=s_c.at[4 * g + 2 * de + kind], recv_sem=r_c.at[8 * kind + head],
            device_id=at(r, 2 * c + g // 2, lax.rem(g, 2), to_e), device_id_type=MESH,
        )

    for g in range(4):
        lanes = slice((g % 2) * TOK, (g % 2) * TOK + TOK)
        total = jnp.sum(l_sc[g // 2, :, lanes], axis=0, keepdims=True)
        res = jnp.transpose(acc[g // 2, :, lanes] / total).astype(BF16)
        cst[g, 0] = res[0:OWN]
        cst[g, 1] = res[OWN:TOK]

        ctx_copy(g, 1, 0).start()

        @pl.when(4 * c + g != p)
        def _():
            ctx_copy(g, 0, 0).start()

        @pl.when(4 * c + g == p)
        def _():
            ctx[0, head] = cst[g, 1 - e]
            ctx[1, head] = cst[g, e]

    for g in range(4):
        ctx_copy(g, 1, 1).start()

        @pl.when(4 * c + g != p)
        def _():
            ctx_copy(g, 0, 1).start()

    def w_copy(quarter):
        start = pl.multiple_of(quarter * 128, 128)
        return pltpu.make_async_remote_copy(
            src_ref=wb.at[1 - e, pl.ds(start, 128)], dst_ref=wb.at[1 - e, pl.ds(start, 128)],
            send_sem=s_w.at[2 + lax.rem(quarter, 2)], recv_sem=r_w.at[quarter],
            device_id=at(r, x, 1 - c, e), device_id_type=MESH,
        )

    for d in range(2):
        w_copy(2 * c + d).wait_recv()
        w_copy(2 * c + d).start()

    send_id.wait_recv()
    upper = (
        lax.broadcasted_iota(jnp.int32, (256, 256), 0) <= lax.broadcasted_iota(jnp.int32, (256, 256), 1)
    ).astype(BF16)
    for n, (src, who) in enumerate(((idr, e), (idm, e), (idm, 1 - e))):
        member = (src[...] == who.astype(F32)).astype(F32)
        member = jnp.concatenate([member, member], axis=0)
        rank = jnp.dot(member.astype(BF16), upper, preferred_element_type=F32)
        rank = jnp.where(member > 0.5, rank - 1.0, -1.0)[0:1]
        slots = lax.broadcasted_iota(jnp.int32, (CAP, 256), 0).astype(F32)
        pm[n] = jnp.where(slots == rank, 1.0, 0.0).astype(BF16)
    nrm[OWN:256] = jnp.zeros((64, D), BF16)

    for one in loads:
        one.wait()
    for d in range(2):
        w_copy(2 * (1 - c) + d).wait_recv()

    def ret_copy(n):
        return pltpu.make_async_remote_copy(
            src_ref=rst.at[n], dst_ref=ret.at[n], send_sem=s_ret.at[n], recv_sem=r_ret.at[n],
            device_id=(s, 1 - e), device_id_type=MESH,
        )

    def expert_pass(kind):
        def ctx_wait(h, carry):
            @pl.when((h != head) | (c != ct))
            def _():
                pltpu.make_async_remote_copy(
                    src_ref=cst.at[0, 0], dst_ref=ctx.at[kind, h], send_sem=s_c.at[0], recv_sem=r_c.at[8 * kind + h],
                    device_id=at(r, x, 1 - c, e), device_id_type=MESH,
                ).wait_recv()

            return carry

        lax.fori_loop(0, 8, ctx_wait, 0)

        def project(n, carry):
            cols = pl.ds(pl.multiple_of(n * WCH, WCH), WCH)
            total = jnp.zeros((OWN, WCH), F32)
            for side in range(2):
                left = jnp.concatenate([ctx[kind, 4 * side + i] for i in range(4)], axis=1)
                total = total + jnp.dot(left, wb[side, :, cols], preferred_element_type=F32)
            att[:, cols] = total
            sq = total * total
            part = sq[:, 0:128]
            for i in range(1, WCH // 128):
                part = part + sq[:, i * 128 : i * 128 + 128]
            return carry + part

        sums = lax.fori_loop(0, NCH, project, jnp.zeros((OWN, 128), F32))
        scale = lax.rsqrt(jnp.sum(sums, axis=1, keepdims=True) * (1.0 / D) + 1e-06)

        def normalize(n, carry):
            cols = pl.ds(pl.multiple_of(n * WCH, WCH), WCH)
            nrm[0:OWN, cols] = (att[:, cols] * scale * gain_ref[:, cols]).astype(BF16)
            rows[:, cols] = jnp.dot(pm[kind], nrm[:, cols], preferred_element_type=F32).astype(BF16)
            return carry

        lax.fori_loop(0, NCH, normalize, 0)

        last = (((1,), (1,)), ((), ()))
        gate = lax.dot_general(rows[...], gwb[...], last, preferred_element_type=F32)
        upp = lax.dot_general(rows[...], uwb[...], last, preferred_element_type=F32)
        hidden = (gate * jax.nn.sigmoid(gate) * upp).astype(BF16)
        for n in range(NCH):
            cols = slice(n * WCH, n * WCH + WCH)
            res = jnp.dot(hidden, dwb[:, cols], preferred_element_type=F32).astype(BF16)
            if kind == 0:
                rst[n] = res
                ret_copy(n).start()
            else:
                own_res[n] = res

    expert_pass(0)
    expert_pass(1)

    for n in range(NCH):
        cols = slice(n * WCH, n * WCH + WCH)
        got = lax.dot_general(pm[1], own_res[n], (((0,), (0,)), ((), ())), preferred_element_type=F32)
        ret_copy(n).wait_recv()
        got = got + lax.dot_general(pm[2], ret[n], (((0,), (0,)), ((), ())), preferred_element_type=F32)
        out_ref[:, cols] = (att[:, cols] + rwc[:, 0:1] * got[0:OWN]).astype(BF16)

    for n in range(NCH):
        ret_copy(n).wait_send()
    for d in (1, 2, 3):
        kv_copy(d).wait_send()
        q_copy(d).wait_send()

    @pl.when(c != ct)
    def _():
        kv_copy(0).wait_send()
        q_copy(0).wait_send()

    def sent(i, carry):
        slot = 8 + 4 * c + i

        @pl.when(slot > 8)
        def _():
            to_next(slot).wait_send()

        @pl.when(c == 0)
        def _():
            to_core1(slot).wait_send()

        return carry

    lax.fori_loop(0, 4, sent, 0)

    def sent_prev(i, carry):
        to_core1(5 + i).wait_send()
        return carry

    lax.fori_loop(0, 3 - 3 * c, sent_prev, 0)

    def sent_ctx(g, carry):
        for kind in range(2):
            ctx_copy(g, 1, kind).wait_send()

        @pl.when(4 * c + g != p)
        def _():
            for kind in range(2):
                ctx_copy(g, 0, kind).wait_send()

        return carry

    lax.fori_loop(0, 4, sent_ctx, 0)
    for one in w_out:
        one.wait_send()
    for d in range(2):
        w_copy(2 * c + d).wait_send()
    send_id.wait_send()


def shards(
    queries, key_heads, value_heads, block_layout, out_weight, norm_gain, expert_ids, route_weight,
    gate_weight, up_weight, down_weight,
):
    vm = pl.BlockSpec(memory_space=pltpu.VMEM)
    anyspace = pl.BlockSpec(memory_space=pl.ANY)
    dma = pltpu.SemaphoreType.DMA
    return pl.pallas_call(
        kernel,
        out_shape=jax.ShapeDtypeStruct((OWN, D), BF16),
        in_specs=[anyspace] * 3 + [pl.BlockSpec(memory_space=pltpu.SMEM), vm, vm, vm] + [anyspace] * 4,
        out_specs=vm,
        scratch_shapes=[
            pltpu.VMEM((TOK, 768), BF16),
            pltpu.VMEM((TOK, 768), BF16),
            pltpu.VMEM((TOK, 512), BF16),
            pltpu.VMEM((4, KVR, 128), BF16),
            pltpu.VMEM((4, QR, 128), BF16),
            pltpu.VMEM((16, KVR, 128), BF16),
            pltpu.VMEM((16, TOK, 128), BF16),
            pltpu.VMEM((4, QR, 128), BF16),
            pltpu.VMEM((2, 256, PAIR), BF16),
            pltpu.VMEM((2, 12, 16, PAIR), BF16),
            pltpu.VMEM((2, 8, PAIR), F32),
            pltpu.VMEM((2, 8, PAIR), F32),
            pltpu.VMEM((2, 128, PAIR), F32),
            pltpu.VMEM((TOK, 256), F32),
            pltpu.VMEM((TOK, 256), F32),
            pltpu.VMEM((TOK, 256), BF16),
            pltpu.VMEM((TOK, 256), BF16),
            pltpu.VMEM((4, 2, OWN, 128), BF16),
            pltpu.VMEM((2, 8, OWN, 128), BF16),
            pltpu.VMEM((2, 512, D), BF16),
            pltpu.VMEM((FF, D), BF16),
            pltpu.VMEM((FF, D), BF16),
            pltpu.VMEM((FF, D), BF16),
            pltpu.VMEM((8, 256), F32),
            pltpu.VMEM((8, 256), F32),
            pltpu.VMEM((8, 256), F32),
            pltpu.VMEM((OWN, 128), F32),
            pltpu.VMEM((OWN, D), F32),
            pltpu.VMEM((256, D), BF16),
            pltpu.VMEM((CAP, D), BF16),
            pltpu.VMEM((NCH, CAP, WCH), BF16),
            pltpu.VMEM((NCH, CAP, WCH), BF16),
            pltpu.VMEM((NCH, CAP, WCH), BF16),
            pltpu.VMEM((3, CAP, 256), BF16),
            dma((7,)),
            dma((4,)), dma((16,)),
            dma((4,)), dma((4,)),
            dma((16,)), dma((8,)),
            dma((16,)), dma((16,)),
            dma((4,)), dma((4,)),
            dma, dma,
            dma((NCH,)), dma((NCH,)),
        ],
        compiler_params=pltpu.CompilerParams(
            collective_id=0, has_side_effects=True, vmem_limit_bytes=60 * 1024 * 1024
        ),
        name="layer",
    )(
        queries, key_heads, value_heads, block_layout, norm_gain.reshape(1, D), expert_ids.reshape(1, OWN),
        route_weight.reshape(1, OWN), out_weight, gate_weight[0].T, up_weight[0].T, down_weight[0],
    )


def solution(mesh):
    in_specs = (
        P("seq", "exp"),
        P("seq", "exp"),
        P("seq", "exp"),
        P("seq", None),
        P("exp", None),
        P(),
        P(("seq", "exp"), None),
        P(("seq", "exp"), None),
        P("exp", None, None),
        P("exp", None, None),
        P("exp", None, None),
    )
    out_specs = P(("seq", "exp"), None)
    return jax.shard_map(shards, mesh=mesh, in_specs=in_specs, out_specs=out_specs, check_vma=False)
```

time: 98 us -> 78.7 us (0.80)
  the two profiles are of different devices: /device:TPU:17 before, /device:TPU:1 now
where the time goes in v2:
time: 78.7 us; the launch traced here: 77.6 us
  Pallas kernels  75.5 us (96%)
  local copies, waits for them, and re-layouts  2.09 us (3%)
    pallas_call x1, Pallas kernels, shards(): pl.pallas_call(kernel, out_shape=jax.ShapeDtypeStruct((OWN, D), BF16), in...  75.5 us
    unnamed x1, local copies, waits for them, and re-layouts  2.09 us

profile of v2, /device:TPU:1, one launch (start us, length us, event | category | flops | bytes accessed | tf_op | source)
XLA Modules:
  0.0 77.6 jit_solution(8085380407293003413)
XLA Ops:
  0.0 75.5 %layer.1 = bf16[192,2048]{1,0:T(8,128)(2,1)} custom-call(bf16[384,768]{1,0:T(8,128)(2,1)} %q_hbm.1, bf16[384,768]{1,0:T(8,128)(2,1)} %k_hbm.1, bf16[384,512]{1,0:T(8,128)(2,1)} %v_hbm.1, s32[3,16]{1,0:T(4,128)} %lay_ref.1, f32[1,2048]{1,0:T(1,128)} %bitcast.13, s32[1,192]{1,0:T(1,128)} %bitcast.14, f32[1,192]{1,0:T(1,128)} %bitcast.15, ...), custom_call_target="tpu_custom_call" | custom-call | tf_op jit(solution)/shard_map/layer/pallas_call | solution.py:553
  75.5 2.1 %copy.13 = bf16[192,2048]{1,0:T(8,128)(2,1)} copy(bf16[192,2048]{1,0:T(8,128)(2,1)} %layer.1) | data formatting | bytes 1572864
